TPU v7x, 8 devices: a whole 2x2x1 slice. The times are simulated.
8 devices in a mesh: dp: 1 (over z), row: 2 (over y), col: 2 (over x), core: 2 (over core).
Axes of the slice: x: 2, y: 2, z: 1, core: 2. Of those that a mesh axis runs over, the one named last changes fastest.
Arguments:
- x: bfloat16 [2048, 896], P(('dp', 'row', 'col', 'core'))
- route_idx: int32 [2048, 8], P(('dp', 'row', 'col', 'core'))
- gates: float32 [2048, 8], P(('dp', 'row', 'col', 'core'))
- w1: bfloat16 [384, 896, 256], P(('row', 'col', 'core'))
- w3: bfloat16 [384, 896, 256], P(('row', 'col', 'core'))
- w2: bfloat16 [384, 256, 896], P(('row', 'col', 'core'))
- dy: bfloat16 [2048, 896], P(('dp', 'row', 'col', 'core'))
Outputs:
- output 1: bfloat16 [2048, 896], P(('dp', 'row', 'col', 'core'))
- output 2: bfloat16 [2048, 896], P(('dp', 'row', 'col', 'core'))
- output 3: float32 [2048, 8], P(('dp', 'row', 'col', 'core'))
- output 4: float32 [384, 896, 256], P(('dp', 'row', 'col', 'core'))
- output 5: float32 [384, 896, 256], P(('dp', 'row', 'col', 'core'))
- output 6: float32 [384, 256, 896], P(('dp', 'row', 'col', 'core'))
All inputs are finite; a program needn't handle non-finite values.
Results may differ from a plain program's by a relative error of at most 0.0104075.
Values are sent between devices in bfloat16 or wider.
A program may use at most 1 GiB of HBM per device.

v0:
```python
import functools

import jax
import jax.numpy as jnp
from jax import lax
from jax.experimental import pallas as pl
from jax.experimental.pallas import tpu as pltpu
from jax.sharding import PartitionSpec as P

F32 = jnp.float32
BF = jnp.bfloat16
CAP = 16
GRP = 16
EB = 4
NS = 3

_T00 = (((0,), (0,)), ((), ()))
_T11 = (((1,), (1,)), ((), ()))


def _dot(a, b, dims=(((1,), (0,)), ((), ()))):
    return lax.dot_general(a, b, dims, preferred_element_type=F32)


def _prep(aux, e0, s, td, el, pos_scr, gate_scr):
    top = aux.shape[0] // 2
    ei = lax.broadcasted_iota(jnp.int32, (el, td), 0).astype(F32)
    hit = jnp.zeros((el, td), F32)
    gate = jnp.zeros((el, td), F32)
    for j in range(top):
        eq = (aux[j:j + 1, :] - e0) == ei
        hit = jnp.where(eq, 1.0, hit)
        gate = jnp.where(eq, aux[top + j:top + j + 1, :], gate)
    before = lax.broadcasted_iota(jnp.int32, (td, td), 0) < lax.broadcasted_iota(jnp.int32, (td, td), 1)
    upper = jnp.where(before, 1.0, 0.0).astype(BF)
    rank = _dot(hit.astype(BF), upper)
    pos_scr[s] = jnp.where(hit > 0.0, rank, -1.0)
    if gate_scr is not None:
        gate_scr[s] = gate


def _mask(pos_scr, s, g, td):
    ci = lax.broadcasted_iota(jnp.int32, (CAP, td), 0).astype(F32)
    pg = pos_scr[s, pl.ds(pl.multiple_of(g * GRP, GRP), GRP), :]
    return jnp.concatenate([jnp.broadcast_to(pg[k:k + 1, :], (CAP, td)) == ci for k in range(GRP)], axis=0)


def _slot_gate(mask, gate_scr, s, g, td):
    gg = gate_scr[s, pl.ds(pl.multiple_of(g * GRP, GRP), GRP), :]
    rep = jnp.concatenate([jnp.broadcast_to(gg[k:k + 1, :], (CAP, td)) for k in range(GRP)], axis=0)
    return jnp.sum(jnp.where(mask, rep, 0.0), axis=1, keepdims=True)


def _onehot(mask):
    return jnp.where(mask, 1.0, 0.0).astype(BF)


def _xor(a, b):
    return a + b - 2 * a * b


def _coords():
    return lax.axis_index('row'), lax.axis_index('col'), lax.axis_index('core')


def _block(r):
    row, col, core = _coords()
    return (_xor(row, r // 4) * 2 + _xor(col, r // 2 % 2)) * 2 + _xor(core, r % 2)


def _device(r):
    row, col, core = _coords()
    return {'row': _xor(row, r // 4), 'col': _xor(col, r // 2 % 2), 'core': _xor(core, r % 2)}


def _e0(el):
    return (_block(0) * el).astype(F32)


def _rows(s, td):
    return pl.ds(pl.multiple_of(s * td, td), td)


class _Gather:
    def __init__(self, own, full, send, recv, local):
        self.own, self.full, self.send, self.recv, self.local = own, full, send, recv, local
        self.h = own.shape[0] // 2
        self.sent = []

    def _half(self, b, h):
        return pl.ds(pl.multiple_of(_block(b) * (2 * self.h) + h * self.h, self.h), self.h)

    def _send(self, d, b, h):
        src = self.own.at[pl.ds(h * self.h, self.h)] if b == 0 else self.full.at[self._half(b, h)]
        c = pltpu.make_async_remote_copy(src_ref=src, dst_ref=self.full.at[self._half(b, h)], send_sem=self.send.at[len(self.sent)],
                                         recv_sem=self.recv.at[b ^ d, h], device_id=_device(d), device_id_type=pl.DeviceIdType.MESH)
        c.start()
        self.sent.append(c)

    def _wait(self, r, h):
        ref = self.full.at[self._half(r, h)]
        pltpu.make_async_remote_copy(src_ref=ref, dst_ref=ref, send_sem=self.send.at[0], recv_sem=self.recv.at[r, h],
                                     device_id=_device(0), device_id_type=pl.DeviceIdType.MESH).wait_recv()

    def start(self):
        self.mine = pltpu.make_async_copy(self.own, self.full.at[_rows(_block(0), 2 * self.h)], self.local)
        for d, h in ((2, 0), (4, 1), (2, 1), (4, 0), (1, 0), (1, 1)):
            self._send(d, 0, h)
        self.mine.start()

    def relay(self):
        self._wait(2, 0)
        self._send(4, 2, 0)
        self._wait(4, 1)
        self._send(2, 4, 1)
        self._send(1, 2, 0)
        self._send(1, 4, 1)

    def cross(self):
        self._wait(2, 1)
        self._send(1, 2, 1)
        self._wait(4, 0)
        self._send(1, 4, 0)
        self._wait(6, 0)
        self._send(1, 6, 0)
        self._wait(6, 1)
        self._send(1, 6, 1)

    def finish(self):
        self.mine.wait()
        for r in (1, 3, 5, 7):
            for h in range(2):
                self._wait(r, h)

    def drain(self):
        for c in self.sent:
            c.wait_send()


class _Weights:
    def __init__(self, hbm, ring, sem):
        self.hbm, self.ring, self.sem = hbm, ring, sem
        self.n = hbm[0].shape[0] // EB

    def _copies(self, it):
        slot = it % NS
        return [pltpu.make_async_copy(w.at[pl.ds(it % self.n * EB, EB)], r.at[slot], self.sem.at[slot, k])
                for k, (w, r) in enumerate(zip(self.hbm, self.ring))]

    def prime(self):
        for it in range(NS):
            for c in self._copies(it):
                c.start()

    def wait(self, it):
        for c in self._copies(it):
            c.wait()
        return it % NS

    def next(self, it):
        @pl.when(it + NS < 2 * self.n)
        def _():
            for c in self._copies(it + NS):
                c.start()


def _greet(relations):
    barrier = pltpu.get_barrier_semaphore()
    for r in relations:
        pl.semaphore_signal(barrier, inc=1, device_id=_device(r), device_id_type=pl.DeviceIdType.MESH)
    pl.semaphore_wait(barrier, len(relations))


def _to_partner(acc, recv, send_sem, recv_sem, q):
    n = recv.shape[1]
    return pltpu.make_async_remote_copy(src_ref=acc.at[_block(7 - 2 * q), pl.ds(0, n)], dst_ref=recv.at[q], send_sem=send_sem.at[q],
                                        recv_sem=recv_sem.at[q], device_id=_device(1), device_id_type=pl.DeviceIdType.MESH)


def _to_chip(src, recv, send_sem, recv_sem, q):
    return pltpu.make_async_remote_copy(src_ref=src.at[q], dst_ref=recv.at[q], send_sem=send_sem.at[q], recv_sem=recv_sem.at[q],
                                        device_id=_device(6 - 2 * q), device_id_type=pl.DeviceIdType.MESH)


def _main_kernel(npd, td, el, aux_ref, x_ref, dy_ref, w1_ref, w3_ref, w2_ref,
                 y_ref, dxd_ref, dxy_ref, dxx_ref, dxs_ref, xe_ref, q_ref, act_ref, du_ref, dv_ref,
                 xa, dya, aux, acc, ur, yr, dr, w1r, w3r, w2r, rg, og, uu, vv, acts, gsg, dgg, pos_scr, gate_scr,
                 sx, rx, sd, rd, sa, ra, sp, rp, sq, rq, sc, rc, lsem, wsem, xsem, qsem, asem, osem, dsem):
    dm = x_ref.shape[1]
    top = aux_ref.shape[0] // 2
    rows = npd * CAP
    ng = el // GRP
    spg = GRP // EB
    nc = npd // 2
    weights = _Weights((w1_ref, w3_ref, w2_ref), (w1r, w3r, w2r), wsem)
    me = _block(0)
    mine = pltpu.make_async_copy(aux_ref, aux.at[me], lsem.at[2])
    mine.start()
    _greet(range(1, npd))
    gx = _Gather(x_ref, xa, sx, rx, lsem.at[0])
    gd = _Gather(dy_ref, dya, sd, rd, lsem.at[1])
    asend = [pltpu.make_async_remote_copy(src_ref=aux_ref, dst_ref=aux.at[me], send_sem=sa.at[r - 1], recv_sem=ra.at[r - 1],
                                          device_id=_device(r), device_id_type=pl.DeviceIdType.MESH) for r in range(1, npd)]
    gx.start()
    for c in asend:
        c.start()
    weights.prime()
    mine.wait()
    for r in range(1, npd):
        ref = aux.at[_block(r)]
        pltpu.make_async_remote_copy(src_ref=ref, dst_ref=ref, send_sem=sa.at[0], recv_sem=ra.at[r - 1],
                                     device_id=_device(0), device_id_type=pl.DeviceIdType.MESH).wait_recv()

    def prep(s, c):
        _prep(aux[s], _e0(el), s, td, el, pos_scr, gate_scr)
        return c
    lax.fori_loop(0, npd, prep, 0)
    gx.relay()
    gd.start()
    gx.cross()
    gx.finish()

    def act_copy(it):
        return pltpu.make_async_copy(acts.at[it % 2], act_ref.at[pl.ds(it * EB, EB)], asem.at[it % 2])

    xout = [pltpu.make_async_copy(rg, xe_ref.at[pl.ds(g * GRP, GRP)], xsem.at[0]) for g in range(ng)]
    for g in range(ng):
        if g > 0:
            xout[g - 1].wait()

        def gather(s, c):
            rg[:, s] = _dot(_onehot(_mask(pos_scr, s, g, td)), xa[_rows(s, td), :]).astype(BF).reshape(GRP, CAP, dm)
            return c
        lax.fori_loop(0, npd, gather, 0)
        xout[g].start()
        if g == 1:
            gd.relay()
        if g == 2:
            gd.cross()

        def experts(k, c):
            it = g * spg + k
            slot = weights.wait(it)

            @pl.when(it >= 2)
            def _():
                act_copy(it - 2).wait()
            for b in range(EB):
                kb = k * EB + b
                xe = rg[kb].reshape(rows, dm)
                u = _dot(xe, w1r[slot, b]).astype(BF)
                v = _dot(xe, w3r[slot, b]).astype(BF)
                uu[g * GRP + kb] = u
                vv[g * GRP + kb] = v
                uf = u.astype(F32)
                act = (uf * jax.nn.sigmoid(uf) * v.astype(F32)).astype(BF)
                acts[it % 2, b] = act
                og[kb] = _dot(act, w2r[slot, b]).astype(BF).reshape(npd, CAP, dm)
            act_copy(it).start()
            weights.next(it)
            return c
        lax.fori_loop(0, spg, experts, 0)

        def combine(s):
            m = _mask(pos_scr, s, g, td)
            gs = _slot_gate(m, gate_scr, s, g, td)
            hi = gs.astype(BF).astype(F32)
            mid = (gs - hi).astype(BF).astype(F32)
            lo = gs - hi - mid
            os = og[:, s].reshape(GRP * CAP, dm)
            y = _dot(jnp.where(m, hi, 0.0).astype(BF), os, _T00)
            y += _dot(jnp.where(m, mid, 0.0).astype(BF), os, _T00)
            y += _dot(jnp.where(m, lo, 0.0).astype(BF), os, _T00)
            return y

        body = pl.ds(0, td)
        if g == 0:
            def first(s, c):
                acc[s, body] = combine(s)
                return c
            lax.fori_loop(0, npd, first, 0)
        elif g < ng - 1:
            def more(s, c):
                acc[s, body] += combine(s)
                return c
            lax.fori_loop(0, npd, more, 0)
        else:
            def other(q, c):
                acc[_block(7 - 2 * q), body] += combine(_block(7 - 2 * q))
                _to_partner(acc, ur, sp, rp, q).start()
                return c
            lax.fori_loop(0, nc, other, 0)

            def ours(q, c):
                s = _block(6 - 2 * q)
                acc[s, body] += combine(s)
                _to_partner(acc, ur, sp, rp, q).wait_recv()
                ur[q] += acc[s, body]

                @pl.when(q < nc - 1)
                def _():
                    _to_chip(ur, yr, sc, rc, q).start()
                return c
            lax.fori_loop(0, nc, ours, 0)
    n = ng * spg
    act_copy(n - 2).wait()
    act_copy(n - 1).wait()
    gd.finish()
    xout[ng - 1].wait()

    outs = []
    for g in range(ng):
        def gather_dy(s, c):
            m = _mask(pos_scr, s, g, td)
            gs = _slot_gate(m, gate_scr, s, g, td)
            gsg[:, s] = jnp.broadcast_to(gs, (GRP * CAP, 128)).reshape(GRP, CAP, 128)
            rg[:, s] = _dot(_onehot(m), dya[_rows(s, td), :]).astype(BF).reshape(GRP, CAP, dm)
            return c
        lax.fori_loop(0, npd, gather_dy, 0)

        def q_copy(k):
            return pltpu.make_async_copy(rg.at[pl.ds(k * EB, EB)], q_ref.at[pl.ds(g * GRP + k * EB, EB)], qsem.at[k])

        def experts_back(k, c):
            it = n + g * spg + k
            slot = weights.wait(it)
            for b in range(EB):
                kb = k * EB + b
                e = g * GRP + kb
                dye = rg[kb].reshape(rows, dm).astype(F32)
                gs = gsg[kb].reshape(rows, 128)
                q = (jnp.concatenate([gs] * (dm // 128), axis=1) * dye).astype(BF)
                rg[kb] = q.reshape(npd, CAP, dm)
                uf = uu[e].astype(F32)
                vf = vv[e].astype(F32)
                sg = jax.nn.sigmoid(uf)
                sl = uf * sg
                act = (sl * vf).astype(BF)
                w2 = w2r[slot, b]
                o = _dot(act, w2).astype(BF).astype(F32)
                dgs = jnp.sum(dye * o, axis=1, keepdims=True)
                dgg[kb] = jnp.broadcast_to(dgs, (rows, 128)).reshape(npd, CAP, 128)
                dact = _dot(q, w2, _T11).astype(BF).astype(F32)
                du = (dact * vf * sg * (1 + uf * (1 - sg))).astype(BF)
                dv = (dact * sl).astype(BF)
                uu[e] = du
                vv[e] = dv
                p = _dot(du, w1r[slot, b], _T11) + _dot(dv, w3r[slot, b], _T11)
                og[kb] = p.astype(BF).reshape(npd, CAP, dm)
            q_copy(k).start()
            weights.next(it)
            return c
        lax.fori_loop(0, spg, experts_back, 0)
        for k, (a, b) in enumerate(((uu, du_ref), (vv, dv_ref))):
            outs.append(pltpu.make_async_copy(a.at[pl.ds(g * GRP, GRP)], b.at[pl.ds(g * GRP, GRP)], osem.at[2 * g + k]))
            outs[-1].start()
        if g == 0:
            for q in range(nc):
                _to_partner(acc, ur, sp, rp, q).wait_send()

            def clear(s, c):
                acc[s, pl.ds(td, top), :] = jnp.zeros((top, dm), F32)
                return c
            lax.fori_loop(0, npd, clear, 0)

        def combine_back(s):
            m = _mask(pos_scr, s, g, td)
            dxs = _dot(_onehot(m), og[:, s].reshape(GRP * CAP, dm), _T00)
            dgr = dgg[:, s].reshape(GRP * CAP, 128)
            dgr = jnp.concatenate([dgr] * (td // 128), axis=1)
            dge = jnp.sum(jnp.where(m, dgr, 0.0).reshape(GRP, CAP, td), axis=1)
            ei = (lax.broadcasted_iota(jnp.int32, (GRP, td), 0) + g * GRP).astype(F32)
            a = aux[s]
            e0 = _e0(el)
            out = [jnp.sum(jnp.where((a[j:j + 1, :] - e0) == ei, dge, 0.0), axis=0, keepdims=True) for j in range(top)]
            acc[s, pl.ds(td, top), pl.ds(0, td)] += jnp.concatenate(out, axis=0)
            return dxs

        if g == 0:
            def first_back(s, c):
                acc[s, body] = combine_back(s)
                return c
            lax.fori_loop(0, npd, first_back, 0)
        elif g < ng - 1:
            def more_back(s, c):
                acc[s, body] += combine_back(s)
                return c
            lax.fori_loop(0, npd, more_back, 0)
        else:
            def other_back(q, c):
                acc[_block(7 - 2 * q), body] += combine_back(_block(7 - 2 * q))
                _to_partner(acc, dr, sq, rq, q).start()
                return c
            lax.fori_loop(0, nc, other_back, 0)

            def ours_back(q, c):
                acc[_block(6 - 2 * q), body] += combine_back(_block(6 - 2 * q))
                return c
            lax.fori_loop(0, nc, ours_back, 0)
        for k in range(spg):
            q_copy(k).wait()
    for q, out in enumerate((dxd_ref, dxy_ref, dxx_ref, dxs_ref)):
        s = _block(6 - 2 * q)
        _to_partner(acc, dr, sq, rq, q).wait_recv()
        acc[s] += dr[q]
        outs.append(pltpu.make_async_copy(acc.at[s], out, dsem.at[q]))
        outs[-1].start()
    y = ur[nc - 1]
    for q in range(nc - 1):
        _to_chip(ur, yr, sc, rc, q).wait_recv()
        y += yr[q]
    y_ref[...] = y.astype(BF)
    for q in range(nc):
        _to_partner(acc, dr, sq, rq, q).wait_send()
    for q in range(nc - 1):
        _to_chip(ur, yr, sc, rc, q).wait_send()
    for c in asend:
        c.wait_send()
    gx.drain()
    gd.drain()
    for c in outs:
        c.wait()


def _dw_kernel(xe_ref, q_ref, act_ref, du_ref, dv_ref, dw1_ref, dw3_ref, dw2_ref):
    rows, dm = act_ref.shape[1], xe_ref.shape[3]
    for b in range(EB):
        xe = xe_ref[b].reshape(rows, dm)
        dw1_ref[b] = _dot(xe, du_ref[b], _T00)
        dw3_ref[b] = _dot(xe, dv_ref[b], _T00)
        dw2_ref[b] = _dot(act_ref[b], q_ref[b].reshape(rows, dm), _T00)


def _per(shape):
    n = len(shape)
    return pl.BlockSpec((EB,) + shape, lambda i: (i,) + (0,) * n)


def solution(mesh):
    ep = ('row', 'col', 'core')
    npd = mesh.shape['row'] * mesh.shape['col'] * mesh.shape['core']
    tspec = P(('dp',) + ep, None)
    wspec = P(ep, None, None)
    gspec = P(('dp',) + ep, None, None)

    def body(x, route_idx, gates, w1, w3, w2, dy):
        td, top = route_idx.shape
        el, dm, fh = w1.shape
        rows = npd * CAP
        tp = td + top
        nc = npd // 2
        aux = jnp.concatenate([route_idx.T.astype(F32), gates.T], axis=0)
        sds = jax.ShapeDtypeStruct
        anyspec = pl.BlockSpec(memory_space=pl.ANY)
        vm = pltpu.VMEM
        dma = pltpu.SemaphoreType.DMA
        slots = vm((GRP, npd, CAP, dm), BF)
        lanes = vm((GRP, npd, CAP, 128), F32)
        hid = vm((el, rows, fh), BF)
        part = sds((tp, dm), F32)
        y, dxd, dxy, dxx, dxs, xe, q, act, du, dv = pl.pallas_call(
            functools.partial(_main_kernel, npd, td, el),
            in_specs=[anyspec] * 6,
            out_specs=[pl.BlockSpec(memory_space=vm)] + [anyspec] * 9,
            out_shape=[sds((td, dm), BF), part, part, part, part, sds((el, npd, CAP, dm), BF), sds((el, npd, CAP, dm), BF),
                       sds((el, rows, fh), BF), sds((el, rows, fh), BF), sds((el, rows, fh), BF)],
            scratch_shapes=[vm((npd * td, dm), BF), vm((npd * td, dm), BF), vm((npd, 2 * top, td), F32),
                            vm((npd, tp, dm), F32), vm((nc, td, dm), F32), vm((nc - 1, td, dm), F32), vm((nc, tp, dm), F32),
                            vm((NS, EB, dm, fh), BF), vm((NS, EB, dm, fh), BF), vm((NS, EB, fh, dm), BF),
                            slots, slots, hid, hid, vm((2, EB, rows, fh), BF), lanes, lanes,
                            vm((npd, el, td), F32), vm((npd, el, td), F32),
                            dma((14,)), dma((8, 2)), dma((14,)), dma((8, 2)), dma((7,)), dma((7,)),
                            dma((nc,)), dma((nc,)), dma((nc,)), dma((nc,)), dma((nc - 1,)), dma((nc - 1,)),
                            dma((3,)), dma((NS, 3)), dma((1,)), dma((GRP // EB,)), dma((2,)), dma((2 * (el // GRP),)), dma((nc,))],
            compiler_params=pltpu.CompilerParams(collective_id=0, has_side_effects=True, vmem_limit_bytes=67043328),
            cost_estimate=pl.CostEstimate(flops=14 * 2 * el * rows * dm * fh, bytes_accessed=200_000_000, transcendentals=0),
            name='moe_main',
        )(aux, x, dy, w1, w3, w2)
        swap = [(0, 1), (1, 0)]
        pd = lax.ppermute(dxd, ('row', 'col'), [(i, 3 - i) for i in range(4)])
        py = lax.ppermute(dxy, 'row', swap)
        px = lax.ppermute(dxx, 'col', swap)
        slotspec = _per((npd, CAP, dm))
        dw1, dw3, dw2 = pl.pallas_call(
            _dw_kernel,
            grid=(el // EB,),
            in_specs=[slotspec, slotspec] + [_per((rows, fh))] * 3,
            out_specs=[_per((dm, fh)), _per((dm, fh)), _per((fh, dm))],
            out_shape=[sds((el, dm, fh), F32), sds((el, dm, fh), F32), sds((el, fh, dm), F32)],
            cost_estimate=pl.CostEstimate(flops=3 * 2 * el * rows * dm * fh, bytes_accessed=165_000_000, transcendentals=0),
            name='moe_dw',
        )(xe, q, act, du, dv)
        dx = dxs + px + py + pd
        return y, dx[:td].astype(BF), dx[td:, :td].T, dw1, dw3, dw2

    return jax.shard_map(body, mesh=mesh, in_specs=(tspec, tspec, tspec, wspec, wspec, wspec, tspec), out_specs=(tspec, tspec, tspec, gspec, gspec, gspec), check_vma=False)
```

profile of v0, /device:TPU:0, one launch (start us, length us, event | category | flops | bytes accessed | tf_op | source)
XLA Modules:
  0.0 186.3 jit_solution(10577820622931639355)
XLA Ops:
  0.6 0.7 convert_bitcast_fusion
  1.3 1.3 pad_maximum_fusion.aux_ref
  2.6 123.6 %moe_main.1 = (bf16[256,896]{1,0:T(8,128)(2,1)}, f32[264,896]{1,0:T(8,128)}, f32[264,896]{1,0:T(8,128)}, f32[264,896]{1,0:T(8,128)}, f32[264,896]{1,0:T(8,128)},...) custom-call(f32[16,256]{1,0:T(8,128)} %pad_maximum_fusion.aux_ref, ...), custom_call_target="tpu_custom_call" | custom-call | flops 39460012032 | bytes 200000000 | tf_op jit(solution)/shard_map/moe_main/pallas_call | solution.py:461
  126.3 0.0 copy-start
  126.3 0.0 copy-start.1
  126.3 1.5 collective-permute-start
  127.8 0.6 collective-permute-start.1
  128.4 1.4 collective-permute-start.2
  129.8 52.8 %moe_dw.1 = (f32[48,896,256]{2,1,0:T(8,128)}, f32[48,896,256]{2,1,0:T(8,128)}, f32[48,256,896]{2,1,0:T(8,128)}) custom-call(bf16[48,8,16,896]{3,2,1,0:T(8,128)(2,1)} %get-tuple-element.24.xe_ref, bf16[48,8,16,896]{3,2,1,0:T(8,128)(2,1)} %get-tuple-element.25.q_ref, bf16[48,128,256]{2,1,0:T(8,128)(2,1)} %get-tuple-element.26.act_ref, ...), custom_call_target="tpu_custom_call" | custom-call | flops 8455716864 | bytes 165000000 | tf_op jit(solution)/shard_map/moe_dw/pallas_call | solution.py:484
  182.6 0.0 collective-permute-done
  182.6 0.0 collective-permute-done.1
  182.6 0.0 collective-permute-done.2
  182.6 0.0 copy-done
  182.6 1.5 add_add_fusion
  184.1 0.6 slice_bitcast_fusion
  184.7 0.8 slice.13
  185.5 0.0 copy-done.1
  185.5 0.8 copy.14
Async XLA Ops:
  126.3 56.3 %copy-start = (f32[264,896]{1,0:T(8,128)S(1)}, f32[264,896]{1,0:T(8,128)}, u32[]{:S(2)}) copy-start(f32[264,896]{1,0:T(8,128)} %get-tuple-element.20) | copy-start | bytes 2838532
  126.3 59.2 %copy-start.1 = (bf16[256,896]{1,0:T(8,128)(2,1)S(1)}, bf16[256,896]{1,0:T(8,128)(2,1)}, u32[]{:S(2)}) copy-start(bf16[256,896]{1,0:T(8,128)(2,1)} %get-tuple-element.38) | copy-start | bytes 1376260
  126.3 56.3 %collective-permute-start = (f32[264,896]{1,0:T(8,128)}, f32[264,896]{1,0:T(8,128)S(1)}, u32[]{:S(2)}, u32[]{:S(2)}) collective-permute-start(f32[264,896]{1,0:T(8,128)} %get-tuple-element.21), channel_id=1, source_target_pairs={{0,2},{2,0},{1,3},{3,1},{4,6},{6,4},{5,7},{7,5}} | collective-permute-start | bytes 2838536 | tf_op jit(solution)/shard_map/ppermute | solution.py:482
  127.8 54.8 %collective-permute-start.1 = (f32[264,896]{1,0:T(8,128)}, f32[264,896]{1,0:T(8,128)S(1)}, u32[]{:S(2)}, u32[]{:S(2)}) collective-permute-start(f32[264,896]{1,0:T(8,128)} %get-tuple-element.22), channel_id=1, source_target_pairs={{0,4},{4,0},{1,5},{5,1},{2,6},{6,2},{3,7},{7,3}} | collective-permute-start | bytes 2838536 | tf_op jit(solution)/shard_map/ppermute | solution.py:481
  128.4 54.2 %collective-permute-start.2 = (f32[264,896]{1,0:T(8,128)}, f32[264,896]{1,0:T(8,128)}, u32[]{:S(2)}, u32[]{:S(2)}) collective-permute-start(f32[264,896]{1,0:T(8,128)} %get-tuple-element.23), channel_id=1, source_target_pairs={{0,6},{2,4},{4,2},{6,0},{1,7},{3,5},{5,3},{7,1}} | collective-permute-start | bytes 2838536 | tf_op jit(solution)/shard_map/ppermute | solution.py:480
where the time goes:
time: 187 us; the launch traced here: 186 us
  Pallas kernels  176 us (94%)
  other arithmetic  3.51 us (2%)
  starting transfers between devices  3.51 us (2%)
  local copies, waits for them, and re-layouts  2.19 us (1%)
    pallas_call x1, Pallas kernels, body(): pl.pallas_call(functools.partial(_main_kernel, npd, td, el), in_specs=[an...  124 us
    pallas_call x1, Pallas kernels, body(): pl.pallas_call(_dw_kernel, grid=(el // EB,), in_specs=[slotspec, slotspec...  52.8 us
  transfers between devices with their start and end apart: 3, of which 0 were waited for; matrix products, arithmetic and copies ran while one was open for 0% of the time, Pallas kernels for 28%

commit v1 on v0

--- a/solution.py
+++ b/solution.py
@@ -73,6 +73,19 @@
     return {'row': _xor(row, r // 4), 'col': _xor(col, r // 2 % 2), 'core': _xor(core, r % 2)}
 
 
+def _slots_of(ref, s, rows):
+    return jnp.concatenate([ref[pl.ds(pl.multiple_of(k * rows + s * CAP, CAP), CAP), :] for k in range(GRP)], axis=0)
+
+
+def _each(n, f, u=8):
+    u = min(u, n)
+    def step(i, c):
+        for j in range(u):
+            f(i * u + j)
+        return c
+    lax.fori_loop(0, n // u, step, 0)
+
+
 def _e0(el):
     return (_block(0) * el).astype(F32)
 
@@ -183,9 +196,9 @@
 
 
 def _main_kernel(npd, td, el, aux_ref, x_ref, dy_ref, w1_ref, w3_ref, w2_ref,
-                 y_ref, dxd_ref, dxy_ref, dxx_ref, dxs_ref, xe_ref, q_ref, act_ref, du_ref, dv_ref,
+                 y_ref, dxd_ref, dxy_ref, dxx_ref, dxs_ref, xe_ref, q_ref, act_ref, du_ref, dv_ref, o_ref,
                  xa, dya, aux, acc, ur, yr, dr, w1r, w3r, w2r, rg, og, uu, vv, acts, gsg, dgg, pos_scr, gate_scr,
-                 sx, rx, sd, rd, sa, ra, sp, rp, sq, rq, sc, rc, lsem, wsem, xsem, qsem, asem, osem, dsem):
+                 sx, rx, sd, rd, sa, ra, sp, rp, sq, rq, sc, rc, lsem, wsem, xsem, qsem, asem, osem, dsem, oosem):
     dm = x_ref.shape[1]
     top = aux_ref.shape[0] // 2
     rows = npd * CAP
@@ -211,10 +224,9 @@
         pltpu.make_async_remote_copy(src_ref=ref, dst_ref=ref, send_sem=sa.at[0], recv_sem=ra.at[r - 1],
                                      device_id=_device(0), device_id_type=pl.DeviceIdType.MESH).wait_recv()
 
-    def prep(s, c):
+    def prep(s):
         _prep(aux[s], _e0(el), s, td, el, pos_scr, gate_scr)
-        return c
-    lax.fori_loop(0, npd, prep, 0)
+    _each(npd, prep)
     gx.relay()
     gd.start()
     gx.cross()
@@ -224,15 +236,18 @@
         return pltpu.make_async_copy(acts.at[it % 2], act_ref.at[pl.ds(it * EB, EB)], asem.at[it % 2])
 
     xout = [pltpu.make_async_copy(rg, xe_ref.at[pl.ds(g * GRP, GRP)], xsem.at[0]) for g in range(ng)]
+    oout = [pltpu.make_async_copy(og, o_ref.at[_rows(g, GRP * rows)], oosem.at[0]) for g in range(ng)]
+    oin = [pltpu.make_async_copy(o_ref.at[_rows(g, GRP * rows)], xa, oosem.at[1]) for g in range(ng)]
     for g in range(ng):
         if g > 0:
             xout[g - 1].wait()
 
-        def gather(s, c):
+        def gather(s):
             rg[:, s] = _dot(_onehot(_mask(pos_scr, s, g, td)), xa[_rows(s, td), :]).astype(BF).reshape(GRP, CAP, dm)
-            return c
-        lax.fori_loop(0, npd, gather, 0)
+        _each(npd, gather)
         xout[g].start()
+        if g > 0:
+            oout[g - 1].wait()
         if g == 1:
             gd.relay()
         if g == 2:
@@ -255,11 +270,12 @@
                 uf = u.astype(F32)
                 act = (uf * jax.nn.sigmoid(uf) * v.astype(F32)).astype(BF)
                 acts[it % 2, b] = act
-                og[kb] = _dot(act, w2r[slot, b]).astype(BF).reshape(npd, CAP, dm)
+                og[_rows(kb, rows), :] = _dot(act, w2r[slot, b]).astype(BF)
             act_copy(it).start()
             weights.next(it)
             return c
         lax.fori_loop(0, spg, experts, 0)
+        oout[g].start()
 
         def combine(s):
             m = _mask(pos_scr, s, g, td)
@@ -267,7 +283,7 @@
             hi = gs.astype(BF).astype(F32)
             mid = (gs - hi).astype(BF).astype(F32)
             lo = gs - hi - mid
-            os = og[:, s].reshape(GRP * CAP, dm)
+            os = _slots_of(og, s, rows)
             y = _dot(jnp.where(m, hi, 0.0).astype(BF), os, _T00)
             y += _dot(jnp.where(m, mid, 0.0).astype(BF), os, _T00)
             y += _dot(jnp.where(m, lo, 0.0).astype(BF), os, _T00)
@@ -275,15 +291,13 @@
 
         body = pl.ds(0, td)
         if g == 0:
-            def first(s, c):
+            def first(s):
                 acc[s, body] = combine(s)
-                return c
-            lax.fori_loop(0, npd, first, 0)
+            _each(npd, first)
         elif g < ng - 1:
-            def more(s, c):
+            def more(s):
                 acc[s, body] += combine(s)
-                return c
-            lax.fori_loop(0, npd, more, 0)
+            _each(npd, more)
         else:
             def other(q, c):
                 acc[_block(7 - 2 * q), body] += combine(_block(7 - 2 * q))
@@ -307,19 +321,23 @@
     act_copy(n - 1).wait()
     gd.finish()
     xout[ng - 1].wait()
+    oout[ng - 1].wait()
+    gx.drain()
+    oin[0].start()
 
     outs = []
     for g in range(ng):
-        def gather_dy(s, c):
+        def gather_dy(s):
             m = _mask(pos_scr, s, g, td)
             gs = _slot_gate(m, gate_scr, s, g, td)
             gsg[:, s] = jnp.broadcast_to(gs, (GRP * CAP, 128)).reshape(GRP, CAP, 128)
             rg[:, s] = _dot(_onehot(m), dya[_rows(s, td), :]).astype(BF).reshape(GRP, CAP, dm)
-            return c
-        lax.fori_loop(0, npd, gather_dy, 0)
+        _each(npd, gather_dy)
 
         def q_copy(k):
             return pltpu.make_async_copy(rg.at[pl.ds(k * EB, EB)], q_ref.at[pl.ds(g * GRP + k * EB, EB)], qsem.at[k])
+
+        oin[g].wait()
 
         def experts_back(k, c):
             it = n + g * spg + k
@@ -335,9 +353,8 @@
                 vf = vv[e].astype(F32)
                 sg = jax.nn.sigmoid(uf)
                 sl = uf * sg
-                act = (sl * vf).astype(BF)
                 w2 = w2r[slot, b]
-                o = _dot(act, w2).astype(BF).astype(F32)
+                o = xa[_rows(kb, rows), :].astype(F32)
                 dgs = jnp.sum(dye * o, axis=1, keepdims=True)
                 dgg[kb] = jnp.broadcast_to(dgs, (rows, 128)).reshape(npd, CAP, 128)
                 dact = _dot(q, w2, _T11).astype(BF).astype(F32)
@@ -346,11 +363,13 @@
                 uu[e] = du
                 vv[e] = dv
                 p = _dot(du, w1r[slot, b], _T11) + _dot(dv, w3r[slot, b], _T11)
-                og[kb] = p.astype(BF).reshape(npd, CAP, dm)
+                og[_rows(kb, rows), :] = p.astype(BF)
             q_copy(k).start()
             weights.next(it)
             return c
         lax.fori_loop(0, spg, experts_back, 0)
+        if g < ng - 1:
+            oin[g + 1].start()
         for k, (a, b) in enumerate(((uu, du_ref), (vv, dv_ref))):
             outs.append(pltpu.make_async_copy(a.at[pl.ds(g * GRP, GRP)], b.at[pl.ds(g * GRP, GRP)], osem.at[2 * g + k]))
             outs[-1].start()
@@ -365,7 +384,7 @@
 
         def combine_back(s):
             m = _mask(pos_scr, s, g, td)
-            dxs = _dot(_onehot(m), og[:, s].reshape(GRP * CAP, dm), _T00)
+            dxs = _dot(_onehot(m), _slots_of(og, s, rows), _T00)
             dgr = dgg[:, s].reshape(GRP * CAP, 128)
             dgr = jnp.concatenate([dgr] * (td // 128), axis=1)
             dge = jnp.sum(jnp.where(m, dgr, 0.0).reshape(GRP, CAP, td), axis=1)
@@ -377,15 +396,13 @@
             return dxs
 
         if g == 0:
-            def first_back(s, c):
+            def first_back(s):
                 acc[s, body] = combine_back(s)
-                return c
-            lax.fori_loop(0, npd, first_back, 0)
+            _each(npd, first_back)
         elif g < ng - 1:
-            def more_back(s, c):
+            def more_back(s):
                 acc[s, body] += combine_back(s)
-                return c
-            lax.fori_loop(0, npd, more_back, 0)
+            _each(npd, more_back)
         else:
             def other_back(q, c):
                 acc[_block(7 - 2 * q), body] += combine_back(_block(7 - 2 * q))
@@ -393,10 +410,9 @@
                 return c
             lax.fori_loop(0, nc, other_back, 0)
 
-            def ours_back(q, c):
+            def ours_back(q):
                 acc[_block(6 - 2 * q), body] += combine_back(_block(6 - 2 * q))
-                return c
-            lax.fori_loop(0, nc, ours_back, 0)
+            _each(nc, ours_back)
         for k in range(spg):
             q_copy(k).wait()
     for q, out in enumerate((dxd_ref, dxy_ref, dxx_ref, dxs_ref)):
@@ -416,7 +432,6 @@
         _to_chip(ur, yr, sc, rc, q).wait_send()
     for c in asend:
         c.wait_send()
-    gx.drain()
     gd.drain()
     for c in outs:
         c.wait()
@@ -458,20 +473,20 @@
         lanes = vm((GRP, npd, CAP, 128), F32)
         hid = vm((el, rows, fh), BF)
         part = sds((tp, dm), F32)
-        y, dxd, dxy, dxx, dxs, xe, q, act, du, dv = pl.pallas_call(
+        y, dxd, dxy, dxx, dxs, xe, q, act, du, dv, _ = pl.pallas_call(
             functools.partial(_main_kernel, npd, td, el),
             in_specs=[anyspec] * 6,
-            out_specs=[pl.BlockSpec(memory_space=vm)] + [anyspec] * 9,
+            out_specs=[pl.BlockSpec(memory_space=vm)] + [anyspec] * 10,
             out_shape=[sds((td, dm), BF), part, part, part, part, sds((el, npd, CAP, dm), BF), sds((el, npd, CAP, dm), BF),
-                       sds((el, rows, fh), BF), sds((el, rows, fh), BF), sds((el, rows, fh), BF)],
+                       sds((el, rows, fh), BF), sds((el, rows, fh), BF), sds((el, rows, fh), BF), sds((el * rows, dm), BF)],
             scratch_shapes=[vm((npd * td, dm), BF), vm((npd * td, dm), BF), vm((npd, 2 * top, td), F32),
                             vm((npd, tp, dm), F32), vm((nc, td, dm), F32), vm((nc - 1, td, dm), F32), vm((nc, tp, dm), F32),
                             vm((NS, EB, dm, fh), BF), vm((NS, EB, dm, fh), BF), vm((NS, EB, fh, dm), BF),
-                            slots, slots, hid, hid, vm((2, EB, rows, fh), BF), lanes, lanes,
+                            slots, vm((GRP * rows, dm), BF), hid, hid, vm((2, EB, rows, fh), BF), lanes, lanes,
                             vm((npd, el, td), F32), vm((npd, el, td), F32),
                             dma((14,)), dma((8, 2)), dma((14,)), dma((8, 2)), dma((7,)), dma((7,)),
                             dma((nc,)), dma((nc,)), dma((nc,)), dma((nc,)), dma((nc - 1,)), dma((nc - 1,)),
-                            dma((3,)), dma((NS, 3)), dma((1,)), dma((GRP // EB,)), dma((2,)), dma((2 * (el // GRP),)), dma((nc,))],
+                            dma((3,)), dma((NS, 3)), dma((1,)), dma((GRP // EB,)), dma((2,)), dma((2 * (el // GRP),)), dma((nc,)), dma((2,))],
             compiler_params=pltpu.CompilerParams(collective_id=0, has_side_effects=True, vmem_limit_bytes=67043328),
             cost_estimate=pl.CostEstimate(flops=14 * 2 * el * rows * dm * fh, bytes_accessed=200_000_000, transcendentals=0),
             name='moe_main',

time: 187 us -> 171 us (0.914)
  Pallas kernels: 176 us -> 161 us
    pallas_call x1, Pallas kernels: 124 us -> 108 us  [body(): pl.pallas_call(functools.partial(_main_kernel, npd, td, el), in_specs=[an...]
  transfers between devices with their start and end apart: 3 -> 3, of which waited for: 0 -> 0; matrix products, arithmetic and copies ran while one was open for 0% -> 0% of each run, Pallas kernels for 28% -> 31%
where the time goes in v1:
time: 171 us; the launch traced here: 170 us
  Pallas kernels  161 us (94%)
  other arithmetic  3.51 us (2%)
  starting transfers between devices  3.51 us (2%)
  local copies, waits for them, and re-layouts  2.19 us (1%)
    pallas_call x1, Pallas kernels, body(): pl.pallas_call(functools.partial(_main_kernel, npd, td, el), in_specs=[an...  108 us
    pallas_call x1, Pallas kernels, body(): pl.pallas_call(_dw_kernel, grid=(el // EB,), in_specs=[slotspec, slotspec...  52.8 us
  transfers between devices with their start and end apart: 3, of which 0 were waited for; matrix products, arithmetic and copies ran while one was open for 0% of the time, Pallas kernels for 31%

profile of v1, /device:TPU:0, one launch (start us, length us, event | category | flops | bytes accessed | tf_op | source)
XLA Modules:
  0.0 170.5 jit_solution(4339885413345350351)
XLA Ops:
  0.6 0.7 convert_bitcast_fusion
  1.3 1.3 pad_maximum_fusion.aux_ref
  2.6 107.8 %moe_main.1 = (bf16[256,896]{1,0:T(8,128)(2,1)}, f32[264,896]{1,0:T(8,128)}, f32[264,896]{1,0:T(8,128)}, f32[264,896]{1,0:T(8,128)}, f32[264,896]{1,0:T(8,128)},...) custom-call(f32[16,256]{1,0:T(8,128)} %pad_maximum_fusion.aux_ref, ...), custom_call_target="tpu_custom_call" | custom-call | flops 39460012032 | bytes 200000000 | tf_op jit(solution)/shard_map/moe_main/pallas_call | solution.py:476
  110.5 0.0 copy-start
  110.5 0.0 copy-start.1
  110.5 1.5 collective-permute-start
  112.0 0.6 collective-permute-start.1
  112.5 1.5 collective-permute-start.2
  114.0 52.8 %moe_dw.1 = (f32[48,896,256]{2,1,0:T(8,128)}, f32[48,896,256]{2,1,0:T(8,128)}, f32[48,256,896]{2,1,0:T(8,128)}) custom-call(bf16[48,8,16,896]{3,2,1,0:T(8,128)(2,1)} %get-tuple-element.24.xe_ref, bf16[48,8,16,896]{3,2,1,0:T(8,128)(2,1)} %get-tuple-element.25.q_ref, bf16[48,128,256]{2,1,0:T(8,128)(2,1)} %get-tuple-element.26.act_ref, ...), custom_call_target="tpu_custom_call" | custom-call | flops 8455716864 | bytes 165000000 | tf_op jit(solution)/shard_map/moe_dw/pallas_call | solution.py:499
  166.7 0.0 collective-permute-done
  166.7 0.0 collective-permute-done.1
  166.7 0.0 collective-permute-done.2
  166.8 0.0 copy-done
  166.8 1.5 add_add_fusion
  168.3 0.6 slice_bitcast_fusion
  168.9 0.8 slice.13
  169.7 0.0 copy-done.1
  169.7 0.8 copy.14
Async XLA Ops:
  110.5 56.3 %copy-start = (f32[264,896]{1,0:T(8,128)S(1)}, f32[264,896]{1,0:T(8,128)}, u32[]{:S(2)}) copy-start(f32[264,896]{1,0:T(8,128)} %get-tuple-element.20) | copy-start | bytes 2838532
  110.5 59.2 %copy-start.1 = (bf16[256,896]{1,0:T(8,128)(2,1)S(1)}, bf16[256,896]{1,0:T(8,128)(2,1)}, u32[]{:S(2)}) copy-start(bf16[256,896]{1,0:T(8,128)(2,1)} %get-tuple-element.38) | copy-start | bytes 1376260
  110.5 56.3 %collective-permute-start = (f32[264,896]{1,0:T(8,128)}, f32[264,896]{1,0:T(8,128)S(1)}, u32[]{:S(2)}, u32[]{:S(2)}) collective-permute-start(f32[264,896]{1,0:T(8,128)} %get-tuple-element.21), channel_id=1, source_target_pairs={{0,2},{2,0},{1,3},{3,1},{4,6},{6,4},{5,7},{7,5}} | collective-permute-start | bytes 2838536 | tf_op jit(solution)/shard_map/ppermute | solution.py:497
  112.0 54.8 %collective-permute-start.1 = (f32[264,896]{1,0:T(8,128)}, f32[264,896]{1,0:T(8,128)S(1)}, u32[]{:S(2)}, u32[]{:S(2)}) collective-permute-start(f32[264,896]{1,0:T(8,128)} %get-tuple-element.22), channel_id=1, source_target_pairs={{0,4},{4,0},{1,5},{5,1},{2,6},{6,2},{3,7},{7,3}} | collective-permute-start | bytes 2838536 | tf_op jit(solution)/shard_map/ppermute | solution.py:496
  112.5 54.2 %collective-permute-start.2 = (f32[264,896]{1,0:T(8,128)}, f32[264,896]{1,0:T(8,128)}, u32[]{:S(2)}, u32[]{:S(2)}) collective-permute-start(f32[264,896]{1,0:T(8,128)} %get-tuple-element.23), channel_id=1, source_target_pairs={{0,6},{2,4},{4,2},{6,0},{1,7},{3,5},{5,3},{7,1}} | collective-permute-start | bytes 2838536 | tf_op jit(solution)/shard_map/ppermute | solution.py:495

commit v2 on v1

--- a/solution.py
+++ b/solution.py
@@ -261,16 +261,14 @@
             def _():
                 act_copy(it - 2).wait()
             for b in range(EB):
-                kb = k * EB + b
-                xe = rg[kb].reshape(rows, dm)
-                u = _dot(xe, w1r[slot, b]).astype(BF)
-                v = _dot(xe, w3r[slot, b]).astype(BF)
-                uu[g * GRP + kb] = u
-                vv[g * GRP + kb] = v
-                uf = u.astype(F32)
-                act = (uf * jax.nn.sigmoid(uf) * v.astype(F32)).astype(BF)
-                acts[it % 2, b] = act
-                og[_rows(kb, rows), :] = _dot(act, w2r[slot, b]).astype(BF)
+                xe = rg[k * EB + b].reshape(rows, dm)
+                uu[it * EB + b] = _dot(xe, w1r[slot, b]).astype(BF)
+                vv[it * EB + b] = _dot(xe, w3r[slot, b]).astype(BF)
+            for b in range(EB):
+                uf = uu[it * EB + b].astype(F32)
+                acts[it % 2, b] = (uf * jax.nn.sigmoid(uf) * vv[it * EB + b].astype(F32)).astype(BF)
+            for b in range(EB):
+                og[_rows(k * EB + b, rows), :] = _dot(acts[it % 2, b], w2r[slot, b]).astype(BF)
             act_copy(it).start()
             weights.next(it)
             return c
@@ -344,25 +342,24 @@
             slot = weights.wait(it)
             for b in range(EB):
                 kb = k * EB + b
-                e = g * GRP + kb
                 dye = rg[kb].reshape(rows, dm).astype(F32)
                 gs = gsg[kb].reshape(rows, 128)
-                q = (jnp.concatenate([gs] * (dm // 128), axis=1) * dye).astype(BF)
-                rg[kb] = q.reshape(npd, CAP, dm)
+                rg[kb] = (jnp.concatenate([gs] * (dm // 128), axis=1) * dye).astype(BF).reshape(npd, CAP, dm)
+                dgs = jnp.sum(dye * xa[_rows(kb, rows), :].astype(F32), axis=1, keepdims=True)
+                dgg[kb] = jnp.broadcast_to(dgs, (rows, 128)).reshape(npd, CAP, 128)
+            for b in range(EB):
+                kb = k * EB + b
+                e = g * GRP + kb
+                dact = _dot(rg[kb].reshape(rows, dm), w2r[slot, b], _T11).astype(BF).astype(F32)
                 uf = uu[e].astype(F32)
                 vf = vv[e].astype(F32)
                 sg = jax.nn.sigmoid(uf)
-                sl = uf * sg
-                w2 = w2r[slot, b]
-                o = xa[_rows(kb, rows), :].astype(F32)
-                dgs = jnp.sum(dye * o, axis=1, keepdims=True)
-                dgg[kb] = jnp.broadcast_to(dgs, (rows, 128)).reshape(npd, CAP, 128)
-                dact = _dot(q, w2, _T11).astype(BF).astype(F32)
-                du = (dact * vf * sg * (1 + uf * (1 - sg))).astype(BF)
-                dv = (dact * sl).astype(BF)
-                uu[e] = du
-                vv[e] = dv
-                p = _dot(du, w1r[slot, b], _T11) + _dot(dv, w3r[slot, b], _T11)
+                uu[e] = (dact * vf * sg * (1 + uf * (1 - sg))).astype(BF)
+                vv[e] = (dact * (uf * sg)).astype(BF)
+            for b in range(EB):
+                kb = k * EB + b
+                e = g * GRP + kb
+                p = _dot(uu[e], w1r[slot, b], _T11) + _dot(vv[e], w3r[slot, b], _T11)
                 og[_rows(kb, rows), :] = p.astype(BF)
             q_copy(k).start()
             weights.next(it)

time: 171 us -> 165 us (0.965)
  Pallas kernels: 161 us -> 155 us
    pallas_call x1, Pallas kernels: 108 us -> 102 us  [body(): pl.pallas_call(functools.partial(_main_kernel, npd, td, el), in_specs=[an...]
  transfers between devices with their start and end apart: 3 -> 3, of which waited for: 0 -> 0; matrix products, arithmetic and copies ran while one was open for 0% -> 0% of each run, Pallas kernels for 31% -> 32%
where the time goes in v2:
time: 165 us
  Pallas kernels  155 us (94%)
  other arithmetic  3.51 us (2%)
  starting transfers between devices  3.51 us (2%)
  local copies, waits for them, and re-layouts  2.19 us (1%)
    pallas_call x1, Pallas kernels, body(): pl.pallas_call(functools.partial(_main_kernel, npd, td, el), in_specs=[an...  102 us
    pallas_call x1, Pallas kernels, body(): pl.pallas_call(_dw_kernel, grid=(el // EB,), in_specs=[slotspec, slotspec...  52.8 us
  transfers between devices with their start and end apart: 3, of which 0 were waited for; matrix products, arithmetic and copies ran while one was open for 0% of the time, Pallas kernels for 32%

profile of v2, /device:TPU:0, one launch (start us, length us, event | category | flops | bytes accessed | tf_op | source)
XLA Modules:
  0.0 165.1 jit_solution(3476095129590588791)
XLA Ops:
  0.6 0.7 convert_bitcast_fusion
  1.3 1.3 pad_maximum_fusion.aux_ref
  2.6 102.5 %moe_main.1 = (bf16[256,896]{1,0:T(8,128)(2,1)}, f32[264,896]{1,0:T(8,128)}, f32[264,896]{1,0:T(8,128)}, f32[264,896]{1,0:T(8,128)}, f32[264,896]{1,0:T(8,128)},...) custom-call(f32[16,256]{1,0:T(8,128)} %pad_maximum_fusion.aux_ref, ...), custom_call_target="tpu_custom_call" | custom-call | flops 39460012032 | bytes 200000000 | tf_op jit(solution)/shard_map/moe_main/pallas_call | solution.py:473
  105.1 0.0 copy-start
  105.1 0.0 copy-start.1
  105.1 1.5 collective-permute-start
  106.6 0.5 collective-permute-start.1
  107.2 1.4 collective-permute-start.2
  108.6 52.8 %moe_dw.1 = (f32[48,896,256]{2,1,0:T(8,128)}, f32[48,896,256]{2,1,0:T(8,128)}, f32[48,256,896]{2,1,0:T(8,128)}) custom-call(bf16[48,8,16,896]{3,2,1,0:T(8,128)(2,1)} %get-tuple-element.24.xe_ref, bf16[48,8,16,896]{3,2,1,0:T(8,128)(2,1)} %get-tuple-element.25.q_ref, bf16[48,128,256]{2,1,0:T(8,128)(2,1)} %get-tuple-element.26.act_ref, ...), custom_call_target="tpu_custom_call" | custom-call | flops 8455716864 | bytes 165000000 | tf_op jit(solution)/shard_map/moe_dw/pallas_call | solution.py:496
  161.4 0.0 collective-permute-done
  161.4 0.0 collective-permute-done.1
  161.4 0.0 collective-permute-done.2
  161.4 0.0 copy-done
  161.4 1.5 add_add_fusion
  162.9 0.6 slice_bitcast_fusion
  163.5 0.8 slice.13
  164.3 0.0 copy-done.1
  164.3 0.8 copy.14
Async XLA Ops:
  105.1 56.3 %copy-start = (f32[264,896]{1,0:T(8,128)S(1)}, f32[264,896]{1,0:T(8,128)}, u32[]{:S(2)}) copy-start(f32[264,896]{1,0:T(8,128)} %get-tuple-element.20) | copy-start | bytes 2838532
  105.1 59.2 %copy-start.1 = (bf16[256,896]{1,0:T(8,128)(2,1)S(1)}, bf16[256,896]{1,0:T(8,128)(2,1)}, u32[]{:S(2)}) copy-start(bf16[256,896]{1,0:T(8,128)(2,1)} %get-tuple-element.38) | copy-start | bytes 1376260
  105.1 56.3 %collective-permute-start = (f32[264,896]{1,0:T(8,128)}, f32[264,896]{1,0:T(8,128)S(1)}, u32[]{:S(2)}, u32[]{:S(2)}) collective-permute-start(f32[264,896]{1,0:T(8,128)} %get-tuple-element.21), channel_id=1, source_target_pairs={{0,2},{2,0},{1,3},{3,1},{4,6},{6,4},{5,7},{7,5}} | collective-permute-start | bytes 2838536 | tf_op jit(solution)/shard_map/ppermute | solution.py:494
  106.6 54.7 %collective-permute-start.1 = (f32[264,896]{1,0:T(8,128)}, f32[264,896]{1,0:T(8,128)S(1)}, u32[]{:S(2)}, u32[]{:S(2)}) collective-permute-start(f32[264,896]{1,0:T(8,128)} %get-tuple-element.22), channel_id=1, source_target_pairs={{0,4},{4,0},{1,5},{5,1},{2,6},{6,2},{3,7},{7,3}} | collective-permute-start | bytes 2838536 | tf_op jit(solution)/shard_map/ppermute | solution.py:493
  107.2 54.2 %collective-permute-start.2 = (f32[264,896]{1,0:T(8,128)}, f32[264,896]{1,0:T(8,128)}, u32[]{:S(2)}, u32[]{:S(2)}) collective-permute-start(f32[264,896]{1,0:T(8,128)} %get-tuple-element.23), channel_id=1, source_target_pairs={{0,6},{2,4},{4,2},{6,0},{1,7},{3,5},{5,3},{7,1}} | collective-permute-start | bytes 2838536 | tf_op jit(solution)/shard_map/ppermute | solution.py:492
